TPU v7x, 32 devices: a whole 2x2x4 slice. The times are simulated.
32 devices in a mesh: outer: 4 (over z), inner: 2 (over x), head: 4 (over y, core).
Axes of the slice: x: 2, y: 2, z: 4, core: 2. Of those that a mesh axis runs over, the one named last changes fastest.
Arguments:
- stored_query_rows: bfloat16 [2048, 32, 128], P(('outer', 'inner'), 'head'), may hold values from -12 to 12
- stored_key_rows: bfloat16 [2048, 8, 128], P(('outer', 'inner'), 'head'), may hold values from -12 to 12
- stored_value_rows: bfloat16 [2048, 8, 128], P(('outer', 'inner'), 'head'), may hold values from -6 to 6
- span_order: int32 [16], replicated, may hold values from 0 to 15, each once
Outputs:
- attended: bfloat16 [2048, 32, 128], P(('outer', 'inner'), 'head')
Inputs may be any that keep to these rules, and one draw needn't show every extreme that they name: `span_order`: a permutation of the sequence's 16 blocks of 128 tokens.
All inputs are finite; a program needn't handle non-finite values.
Results may differ from a plain program's by a relative error of at most 0.0075.
Values may be sent and summed in bfloat16 or wider, within the bound.
A program may use at most 128 MiB of HBM per device.

v0:
```python
import functools
import math

import jax
import jax.numpy as jnp
from jax import lax
from jax.experimental import pallas as pl
from jax.experimental.pallas import tpu as pltpu
from jax.sharding import PartitionSpec as P

MESH = pl.DeviceIdType.MESH
MASKED = -1e30
TILE = 512
CHUNKS = 4


def kernel(
    n_outer,
    n_inner,
    heads,
    span_hbm,
    q_ref,
    kv_ref,
    o_ref,
    span_ref,
    span_sem,
    wide_ref,
    held,
    top_ref,
    sum_ref,
    acc_ref,
    send_up,
    send_down,
    send_across,
    send_buddy,
    recv_sem,
):
    rows, width = q_ref.shape
    kv_rows = kv_ref.shape[0]
    pair = kv_ref.shape[1] // 2
    span = kv_rows // 2
    chunk = kv_rows // CHUNKS
    tiles = rows // TILE
    factor = math.log2(math.e) / math.sqrt(width)
    outer = lax.axis_index("outer")
    inner = lax.axis_index("inner")
    use_buddy = n_outer % 2 == 0 and n_outer > 2
    buddy = outer + 1 - 2 * lax.rem(outer, 2) if use_buddy else n_outer

    spans = pltpu.make_async_copy(span_hbm, span_ref, span_sem)
    spans.start()

    barrier = pltpu.get_barrier_semaphore()

    @pl.when(outer > 0)
    def _():
        pl.semaphore_signal(barrier, inc=1, device_id={"outer": outer - 1}, device_id_type=MESH)

    @pl.when(outer < n_outer - 1)
    def _():
        pl.semaphore_signal(barrier, inc=1, device_id={"outer": outer + 1}, device_id_type=MESH)

    for step in range(1, n_inner):
        peer = lax.rem(inner + step, n_inner)
        pl.semaphore_signal(barrier, inc=1, device_id={"inner": peer}, device_id_type=MESH)

    ends = jnp.minimum(outer, 1) + jnp.minimum(n_outer - 1 - outer, 1)
    pl.semaphore_wait(barrier, n_inner - 1 + ends)

    def copy_of(source, src_outer, src_inner, part, send_sem, target):
        return pltpu.make_async_remote_copy(
            src_ref=source.at[pl.ds(part * chunk, chunk)],
            dst_ref=held.at[src_outer, src_inner, pl.ds(part * chunk, chunk)],
            send_sem=send_sem,
            recv_sem=recv_sem.at[src_outer, src_inner, part],
            device_id=target,
            device_id_type=MESH,
        )

    def up(source, src_outer, part):
        return copy_of(
            source, src_outer, inner, part, send_up.at[src_outer, part], {"outer": outer + 1}
        )

    def down(source, src_outer, part):
        return copy_of(
            source, src_outer, inner, part, send_down.at[src_outer, part], {"outer": outer - 1}
        )

    def across(source, src_outer, part, step):
        peer = lax.rem(inner + step, n_inner)
        return copy_of(
            source,
            src_outer,
            inner,
            part,
            send_across.at[src_outer, part, step - 1],
            {"inner": peer},
        )

    def pass_on(source, src_outer, part, act):
        @pl.when(jnp.logical_and(src_outer <= outer, outer < n_outer - 1))
        def _():
            act(up(source, src_outer, part))

        @pl.when(jnp.logical_and(src_outer >= outer, outer > 0))
        def _():
            act(down(source, src_outer, part))

        @pl.when(jnp.logical_or(src_outer != buddy, part < CHUNKS // 2))
        def _():
            for step in range(1, n_inner):
                act(across(source, src_outer, part, step))

    def to_buddy(act):
        def one(step, carry):
            src_inner = lax.rem(inner + step, n_inner)
            for part in range(CHUNKS // 2, CHUNKS):
                act(
                    copy_of(
                        held.at[outer, src_inner],
                        outer,
                        src_inner,
                        part,
                        send_buddy.at[step - 1, part],
                        {"outer": buddy},
                    )
                )
            return carry

        lax.fori_loop(1, n_inner, one, 0)

    def arrived(src_outer, src_inner, part):
        place = held.at[src_outer, src_inner, pl.ds(part * chunk, chunk)]
        pltpu.make_async_remote_copy(
            src_ref=place,
            dst_ref=place,
            send_sem=recv_sem.at[src_outer, src_inner, part],
            recv_sem=recv_sem.at[src_outer, src_inner, part],
            device_id={"inner": lax.rem(inner + 1, n_inner)},
            device_id_type=MESH,
        ).wait_recv()

    for part in range(CHUNKS):
        pass_on(kv_ref, outer, part, lambda copy: copy.start())

    spans.wait()

    row_head = lax.rem(lax.broadcasted_iota(jnp.int32, (TILE, width), 0), heads)
    first_head = row_head < heads // 2
    keep_first = jnp.where(first_head, 1.0, 0.0).astype(q_ref.dtype)
    keep_second = jnp.where(first_head, 0.0, 1.0).astype(q_ref.dtype)
    here = (outer * n_inner + inner) * 2
    lane = lax.broadcasted_iota(jnp.int32, (TILE, kv_rows), 1)

    def attend(block, value):
        pv = jnp.dot(block.astype(jnp.bfloat16), value, preferred_element_type=jnp.float32)
        return jnp.where(first_head, pv[:, :width], pv[:, width:])

    def scores_of(wide, key):
        return lax.dot_general(
            wide, key, (((1,), (1,)), ((), ())), preferred_element_type=jnp.float32
        )

    def at(index):
        return pl.ds(index * TILE, TILE)

    def own_scores(index):
        query = q_ref[at(index), :]
        wide = jnp.concatenate([query * keep_first, query * keep_second], axis=1)
        wide_ref[at(index), :] = wide
        return scores_of(wide, kv_ref[:, :pair])

    def visit_own():
        row = lax.broadcasted_iota(jnp.int32, (TILE, kv_rows), 0)
        anchor = jnp.where(lane < span, span_ref[here], span_ref[here + 1])
        ahead = anchor * span + lax.rem(lane, span) - row // heads
        scores = own_scores(0)
        for index in range(tiles):
            following = own_scores(index + 1) if index + 1 < tiles else None
            q_block = index // (tiles // 2)
            q_offset = (index - q_block * (tiles // 2)) * TILE // heads
            allowed = ahead <= span_ref[here + q_block] * span + q_offset
            scores = jnp.where(allowed, scores, MASKED)
            top = jnp.max(scores, axis=1, keepdims=True)
            weights = jnp.exp2((scores - top) * factor)
            top_ref[at(index), :] = jnp.broadcast_to(top, (TILE, width))
            sum_ref[at(index), :] = weights[:, :width] + weights[:, width:]
            acc_ref[at(index), :] = attend(weights, kv_ref[:, pair:])
            scores = following

    visit_own()

    def visit(src_outer, src_inner):
        base = (src_outer * n_inner + src_inner) * 2
        anchors = [span_ref[base], span_ref[base + 1]]
        place = held.at[src_outer, src_inner]

        def settle_sum(index, rescale, added):
            acc_ref[at(index), :] = acc_ref[at(index), :] * rescale + added

        scores = scores_of(wide_ref[at(0), :], place[:, :pair])
        waiting = None
        for index in range(tiles):
            following = None
            if index + 1 < tiles:
                following = scores_of(wide_ref[at(index + 1), :], place[:, :pair])
            q_anchor = span_ref[here + index // (tiles // 2)]
            bias = [jnp.where(anchor < q_anchor, 0.0, MASKED) for anchor in anchors]
            left = scores[:, :width] + bias[0]
            right = scores[:, width:] + bias[1]
            old = top_ref[at(index), :]
            top = jnp.maximum(old, jnp.max(jnp.maximum(left, right), axis=1, keepdims=True))
            rescale = jnp.exp2((old - top) * factor)
            left = jnp.exp2((left - top) * factor)
            right = jnp.exp2((right - top) * factor)
            top_ref[at(index), :] = top
            sum_ref[at(index), :] = sum_ref[at(index), :] * rescale + (left + right)
            weights = jnp.concatenate([left, right], axis=1)
            added = attend(weights, place[:, pair:])
            if waiting is not None:
                settle_sum(*waiting)
            waiting = (index, rescale, added)
            scores = following
        settle_sum(*waiting)

    below = jnp.minimum(outer, n_outer - 1 - outer)

    def nth(step):
        paired = step <= 2 * below
        distance = jnp.where(paired, (step + 1) // 2, step - below)
        upward = jnp.where(
            paired, lax.rem(step, 2) == 0, outer < n_outer - 1 - outer
        )
        return jnp.where(upward, outer + distance, outer - distance)

    def from_inner(src_outer):
        def one(step, carry):
            src_inner = lax.rem(inner + step, n_inner)
            for part in range(CHUNKS):
                arrived(src_outer, src_inner, part)
            visit(src_outer, src_inner)
            return carry

        lax.fori_loop(1, n_inner, one, 0)

    def take(src_outer, parts):
        for part in parts:
            arrived(src_outer, inner, part)
            pass_on(held.at[src_outer, inner], src_outer, part, lambda copy: copy.start())

    def line_step(step, carry):
        take(nth(step), range(CHUNKS // 2))

        @pl.when(step > 1)
        def _():
            visit(nth(step - 1), inner)

        take(nth(step), range(CHUNKS // 2, CHUNKS))

        @pl.when(jnp.logical_and(step > 1, nth(step - 2) != buddy))
        def _():
            from_inner(nth(step - 2))

        return carry

    lax.fori_loop(1, n_outer, line_step, 0)
    if use_buddy:
        to_buddy(lambda copy: copy.start())
    visit(nth(n_outer - 1), inner)

    def last_step(step, carry):
        src_outer = jnp.where(step == 0, nth(n_outer - 2), nth(n_outer - 1))
        if use_buddy:
            src_outer = jnp.where(step == 1, buddy, src_outer)
            wanted = jnp.logical_or(step == 1, src_outer != buddy)
        else:
            wanted = step != 1

        @pl.when(wanted)
        def _():
            from_inner(src_outer)

        return carry

    lax.fori_loop(0, 3, last_step, 0)

    for index in range(tiles):
        total = jnp.sum(sum_ref[at(index), :], axis=1, keepdims=True)
        o_ref[at(index), :] = (acc_ref[at(index), :] / total).astype(o_ref.dtype)

    def settle(src_outer, carry):
        for part in range(CHUNKS):
            pass_on(kv_ref, src_outer, part, lambda copy: copy.wait_send())
        return carry

    lax.fori_loop(0, n_outer, settle, 0)
    if use_buddy:
        to_buddy(lambda copy: copy.wait_send())


def solution(mesh):
    n_outer, n_inner = mesh.shape["outer"], mesh.shape["inner"]

    def body(query, key, value, span_order):
        kv_rows, groups, width = key.shape
        heads = query.shape[1]
        rows = query.shape[0] * heads
        kv = jnp.concatenate(
            [key.reshape(kv_rows, groups * width), value.reshape(kv_rows, groups * width)], axis=1
        )
        vmem = pl.BlockSpec(memory_space=pltpu.VMEM)
        out = pl.pallas_call(
            functools.partial(kernel, n_outer, n_inner, heads),
            out_shape=jax.ShapeDtypeStruct((rows, width), jnp.bfloat16),
            in_specs=[pl.BlockSpec(memory_space=pltpu.HBM), vmem, vmem],
            out_specs=vmem,
            scratch_shapes=[
                pltpu.SMEM(span_order.shape, jnp.int32),
                pltpu.SemaphoreType.DMA,
                pltpu.VMEM((rows, groups * width), jnp.bfloat16),
                pltpu.VMEM((n_outer, n_inner) + kv.shape, jnp.bfloat16),
                pltpu.VMEM((rows, width), jnp.float32),
                pltpu.VMEM((rows, width), jnp.float32),
                pltpu.VMEM((rows, width), jnp.float32),
                pltpu.SemaphoreType.DMA((n_outer, CHUNKS)),
                pltpu.SemaphoreType.DMA((n_outer, CHUNKS)),
                pltpu.SemaphoreType.DMA((n_outer, CHUNKS, max(n_inner - 1, 1))),
                pltpu.SemaphoreType.DMA((max(n_inner - 1, 1), CHUNKS)),
                pltpu.SemaphoreType.DMA((n_outer, n_inner, CHUNKS)),
            ],
            compiler_params=pltpu.CompilerParams(
                collective_id=0, has_side_effects=True, vmem_limit_bytes=48 * 1024 * 1024
            ),
        )(span_order, query.reshape(rows, width), kv)
        return out.reshape(query.shape)

    placed = P(("outer", "inner"), "head", None)
    return jax.shard_map(
        body,
        mesh=mesh,
        in_specs=(placed, placed, placed, P()),
        out_specs=placed,
        check_vma=False,
    )
```

profile of v0, /device:TPU:0, one launch (start us, length us, event | category | flops | bytes accessed | tf_op | source)
XLA Modules:
  0.0 32.2 jit_solution(6487831396317655409)
XLA Ops:
  0.0 0.0 copy-start
  0.0 1.1 %copy_bitcast_fusion = (bf16[256,256]{1,0:T(8,128)(2,1)S(1)}, bf16[256,256]{1,0:T(8,128)(2,1)S(1)}) fusion(bf16[32,8,2,128]{3,2,1,0:T(2,128)(2,1)} %bitcast.10, bf16[32,8,2,128]{3,2,1,0:T(2,128)(2,1)} %bitcast.11), kind=kLoop, calls=%fused_computation.1 | loop fusion | bytes 524288 | tf_op jit(solution)/shard_map/reshape | solution.py:310
  1.1 0.0 copy-start.1
  1.1 0.1 copy-done
  1.2 0.6 %copy-done.1 = s32[16]{0:T(128)S(1)} copy-done((s32[16]{0:T(128)S(1)}, s32[16]{0:T(128)}, u32[]{:S(2)}) %copy-start.1) | copy-done | bytes 88
  1.7 29.6 %shard_map.46 = bf16[2048,128]{1,0:T(8,128)(2,1)S(1)} custom-call(s32[16]{0:T(128)S(1)} %copy-done.1, bf16[2048,128]{1,0:T(8,128)(2,1)S(1)} %bitcast.9, bf16[256,512]{1,0:T(8,128)(2,1)S(1)} %pad_maximum_fusion.kv_ref), custom_call_target="tpu_custom_call" | custom-call | tf_op jit(solution)/shard_map/pallas_call | solution.py:313
  31.4 0.8 %copy.10 = bf16[256,8,128]{2,1,0:T(8,128)(2,1)} copy(bf16[256,8,128]{2,1,0:T(8,128)(2,1)S(1)} %bitcast.8) | data formatting | bytes 1048576
  (1 shorter events, 0.0 us)
Async XLA Ops:
  0.0 1.2 %copy-start = (bf16[256,8,128]{2,1,0:T(8,128)(2,1)S(1)}, bf16[256,8,128]{2,1,0:T(8,128)(2,1)}, u32[]{:S(2)}) copy-start(bf16[256,8,128]{2,1,0:T(8,128)(2,1)} %param.4) | copy-start | bytes 1572868
  1.1 0.7 %copy-start.1 = (s32[16]{0:T(128)S(1)}, s32[16]{0:T(128)}, u32[]{:S(2)}) copy-start(s32[16]{0:T(128)} %span_hbm.1) | copy-start | bytes 196
where the time goes:
time: 32.3 us; the launch traced here: 32.2 us
  Pallas kernels  29.6 us (92%)
  local copies, waits for them, and re-layouts  2.5 us (8%)
    pallas_call x1, Pallas kernels, body(): pl.pallas_call(functools.partial(kernel, n_outer, n_inner, heads), out_sh...  29.6 us
    unnamed x5, local copies, waits for them, and re-layouts  1.44 us
    reshape x1, local copies, waits for them, and re-layouts, body(): value.reshape(kv_rows, groups * width)  1.06 us

commit v1 on v0

--- a/solution.py
+++ b/solution.py
@@ -32,7 +32,7 @@
     send_up,
     send_down,
     send_across,
-    send_buddy,
+    send_far,
     recv_sem,
 ):
     rows, width = q_ref.shape
@@ -44,8 +44,8 @@
     factor = math.log2(math.e) / math.sqrt(width)
     outer = lax.axis_index("outer")
     inner = lax.axis_index("inner")
-    use_buddy = n_outer % 2 == 0 and n_outer > 2
-    buddy = outer + 1 - 2 * lax.rem(outer, 2) if use_buddy else n_outer
+    far_halves = n_inner == 2 and n_outer > 2
+    last = n_outer - 1
 
     spans = pltpu.make_async_copy(span_hbm, span_ref, span_sem)
     spans.start()
@@ -98,8 +98,16 @@
             {"inner": peer},
         )
 
+    def is_far(src_outer):
+        return jnp.logical_or(src_outer == 0, src_outer == last)
+
+    def crosses(src_outer, part):
+        if not far_halves or part < CHUNKS // 2:
+            return jnp.bool_(True)
+        return jnp.logical_or(src_outer == outer, jnp.logical_not(is_far(src_outer)))
+
     def pass_on(source, src_outer, part, act):
-        @pl.when(jnp.logical_and(src_outer <= outer, outer < n_outer - 1))
+        @pl.when(jnp.logical_and(src_outer <= outer, outer < last))
         def _():
             act(up(source, src_outer, part))
 
@@ -107,28 +115,30 @@
         def _():
             act(down(source, src_outer, part))
 
-        @pl.when(jnp.logical_or(src_outer != buddy, part < CHUNKS // 2))
+        @pl.when(crosses(src_outer, part))
         def _():
             for step in range(1, n_inner):
                 act(across(source, src_outer, part, step))
 
-    def to_buddy(act):
-        def one(step, carry):
-            src_inner = lax.rem(inner + step, n_inner)
-            for part in range(CHUNKS // 2, CHUNKS):
-                act(
-                    copy_of(
-                        held.at[outer, src_inner],
-                        outer,
-                        src_inner,
-                        part,
-                        send_buddy.at[step - 1, part],
-                        {"outer": buddy},
-                    )
+    def far_on(src_outer, part, act):
+        other = n_inner - 1 - inner
+        source = held.at[src_outer, other]
+
+        @pl.when(jnp.logical_and(src_outer == 0, outer < last))
+        def _():
+            act(
+                copy_of(
+                    source, 0, other, part, send_far.at[0, part], {"outer": outer + 1}
                 )
-            return carry
-
-        lax.fori_loop(1, n_inner, one, 0)
+            )
+
+        @pl.when(jnp.logical_and(src_outer == last, outer > 0))
+        def _():
+            act(
+                copy_of(
+                    source, last, other, part, send_far.at[1, part], {"outer": outer - 1}
+                )
+            )
 
     def arrived(src_outer, src_inner, part):
         place = held.at[src_outer, src_inner, pl.ds(part * chunk, chunk)]
@@ -224,66 +234,74 @@
             scores = following
         settle_sum(*waiting)
 
-    below = jnp.minimum(outer, n_outer - 1 - outer)
-
-    def nth(step):
-        paired = step <= 2 * below
-        distance = jnp.where(paired, (step + 1) // 2, step - below)
-        upward = jnp.where(
-            paired, lax.rem(step, 2) == 0, outer < n_outer - 1 - outer
-        )
-        return jnp.where(upward, outer + distance, outer - distance)
-
-    def from_inner(src_outer):
-        def one(step, carry):
-            src_inner = lax.rem(inner + step, n_inner)
-            for part in range(CHUNKS):
-                arrived(src_outer, src_inner, part)
-            visit(src_outer, src_inner)
+    first_half, second_half = range(CHUNKS // 2), range(CHUNKS // 2, CHUNKS)
+
+    def take(step, parts):
+        for part in parts:
+            for side in (1, -1):
+                src_outer = outer + side * step
+
+                @pl.when(jnp.logical_and(src_outer >= 0, src_outer < n_outer))
+                def _():
+                    arrived(src_outer, inner, part)
+                    pass_on(
+                        held.at[src_outer, inner], src_outer, part, lambda copy: copy.start()
+                    )
+
+                if far_halves and part >= CHUNKS // 2:
+
+                    @pl.when(src_outer == (n_outer if side == 1 else -1))
+                    def _():
+                        end = last if side == 1 else 0
+                        arrived(end, n_inner - 1 - inner, part)
+                        far_on(end, part, lambda copy: copy.start())
+
+    def visit_sides(distance, other):
+        def one(side, carry):
+            src_outer = outer + (1 - 2 * side) * distance
+
+            @pl.when(
+                jnp.logical_and(
+                    jnp.logical_and(src_outer >= 0, src_outer < n_outer),
+                    jnp.logical_and(distance >= 0, jnp.logical_or(distance > 0, side == 0)),
+                )
+            )
+            def _():
+                if not other:
+                    visit(src_outer, inner)
+                else:
+
+                    def of_inner(step, carry):
+                        src_inner = lax.rem(inner + step, n_inner)
+                        for part in range(CHUNKS):
+                            if far_halves and part >= CHUNKS // 2:
+
+                                @pl.when(jnp.logical_not(is_far(src_outer)))
+                                def _():
+                                    arrived(src_outer, src_inner, part)
+                            else:
+                                arrived(src_outer, src_inner, part)
+                        visit(src_outer, src_inner)
+                        return carry
+
+                    lax.fori_loop(1, n_inner, of_inner, 0)
+
             return carry
 
-        lax.fori_loop(1, n_inner, one, 0)
-
-    def take(src_outer, parts):
-        for part in parts:
-            arrived(src_outer, inner, part)
-            pass_on(held.at[src_outer, inner], src_outer, part, lambda copy: copy.start())
+        lax.fori_loop(0, 2, one, 0)
 
     def line_step(step, carry):
-        take(nth(step), range(CHUNKS // 2))
-
         @pl.when(step > 1)
         def _():
-            visit(nth(step - 1), inner)
-
-        take(nth(step), range(CHUNKS // 2, CHUNKS))
-
-        @pl.when(jnp.logical_and(step > 1, nth(step - 2) != buddy))
-        def _():
-            from_inner(nth(step - 2))
-
+            visit_sides(step - 1, False)
+
+        take(step, first_half)
+        visit_sides(step - 2, True)
+        take(step, second_half)
         return carry
 
-    lax.fori_loop(1, n_outer, line_step, 0)
-    if use_buddy:
-        to_buddy(lambda copy: copy.start())
-    visit(nth(n_outer - 1), inner)
-
-    def last_step(step, carry):
-        src_outer = jnp.where(step == 0, nth(n_outer - 2), nth(n_outer - 1))
-        if use_buddy:
-            src_outer = jnp.where(step == 1, buddy, src_outer)
-            wanted = jnp.logical_or(step == 1, src_outer != buddy)
-        else:
-            wanted = step != 1
-
-        @pl.when(wanted)
-        def _():
-            from_inner(src_outer)
-
-        return carry
-
-    lax.fori_loop(0, 3, last_step, 0)
+    lax.fori_loop(1, n_outer + 1, line_step, 0)
+    visit_sides(n_outer - 1, True)
 
     for index in range(tiles):
         total = jnp.sum(sum_ref[at(index), :], axis=1, keepdims=True)
@@ -295,8 +313,10 @@
         return carry
 
     lax.fori_loop(0, n_outer, settle, 0)
-    if use_buddy:
-        to_buddy(lambda copy: copy.wait_send())
+    if far_halves:
+        for part in second_half:
+            for end in (0, last):
+                far_on(end, part, lambda copy: copy.wait_send())
 
 
 def solution(mesh):
@@ -326,7 +346,7 @@
                 pltpu.SemaphoreType.DMA((n_outer, CHUNKS)),
                 pltpu.SemaphoreType.DMA((n_outer, CHUNKS)),
                 pltpu.SemaphoreType.DMA((n_outer, CHUNKS, max(n_inner - 1, 1))),
-                pltpu.SemaphoreType.DMA((max(n_inner - 1, 1), CHUNKS)),
+                pltpu.SemaphoreType.DMA((2, CHUNKS)),
                 pltpu.SemaphoreType.DMA((n_outer, n_inner, CHUNKS)),
             ],
             compiler_params=pltpu.CompilerParams(

time: 32.3 us -> 32.1 us (level)
  no operation moved by 1% of the time
where the time goes in v1:
time: 32.1 us; the launch traced here: 31.9 us
  Pallas kernels  29.4 us (92%)
  local copies, waits for them, and re-layouts  2.5 us (8%)
    pallas_call x1, Pallas kernels, body(): pl.pallas_call(functools.partial(kernel, n_outer, n_inner, heads), out_sh...  29.4 us
    unnamed x5, local copies, waits for them, and re-layouts  1.44 us
    reshape x1, local copies, waits for them, and re-layouts, body(): value.reshape(kv_rows, groups * width)  1.06 us

profile of v1, /device:TPU:0, one launch (start us, length us, event | category | flops | bytes accessed | tf_op | source)
XLA Modules:
  0.0 31.9 jit_solution(11516602565007906862)
XLA Ops:
  0.0 0.0 copy-start
  0.0 1.1 %copy_bitcast_fusion = (bf16[256,256]{1,0:T(8,128)(2,1)S(1)}, bf16[256,256]{1,0:T(8,128)(2,1)S(1)}) fusion(bf16[32,8,2,128]{3,2,1,0:T(2,128)(2,1)} %bitcast.10, bf16[32,8,2,128]{3,2,1,0:T(2,128)(2,1)} %bitcast.11), kind=kLoop, calls=%fused_computation.1 | loop fusion | bytes 524288 | tf_op jit(solution)/shard_map/reshape | solution.py:330
  1.1 0.0 copy-start.1
  1.1 0.1 copy-done
  1.2 0.6 %copy-done.1 = s32[16]{0:T(128)S(1)} copy-done((s32[16]{0:T(128)S(1)}, s32[16]{0:T(128)}, u32[]{:S(2)}) %copy-start.1) | copy-done | bytes 88
  1.7 29.4 %shard_map.46 = bf16[2048,128]{1,0:T(8,128)(2,1)S(1)} custom-call(s32[16]{0:T(128)S(1)} %copy-done.1, bf16[2048,128]{1,0:T(8,128)(2,1)S(1)} %bitcast.9, bf16[256,512]{1,0:T(8,128)(2,1)S(1)} %pad_maximum_fusion.kv_ref), custom_call_target="tpu_custom_call" | custom-call | tf_op jit(solution)/shard_map/pallas_call | solution.py:333
  31.1 0.8 %copy.10 = bf16[256,8,128]{2,1,0:T(8,128)(2,1)} copy(bf16[256,8,128]{2,1,0:T(8,128)(2,1)S(1)} %bitcast.8) | data formatting | bytes 1048576
  (1 shorter events, 0.0 us)
Async XLA Ops:
  0.0 1.2 %copy-start = (bf16[256,8,128]{2,1,0:T(8,128)(2,1)S(1)}, bf16[256,8,128]{2,1,0:T(8,128)(2,1)}, u32[]{:S(2)}) copy-start(bf16[256,8,128]{2,1,0:T(8,128)(2,1)} %param.4) | copy-start | bytes 1572868
  1.1 0.7 %copy-start.1 = (s32[16]{0:T(128)S(1)}, s32[16]{0:T(128)}, u32[]{:S(2)}) copy-start(s32[16]{0:T(128)} %span_hbm.1) | copy-start | bytes 196

commit v2 on v1

--- a/solution.py
+++ b/solution.py
@@ -10,7 +10,7 @@
 
 MESH = pl.DeviceIdType.MESH
 MASKED = -1e30
-TILE = 512
+VMEM_LIMIT = 48 * 1024 * 1024
 CHUNKS = 4
 
 
@@ -19,36 +19,50 @@
     n_inner,
     heads,
     span_hbm,
-    q_ref,
-    kv_ref,
+    q_hbm,
+    key_hbm,
+    value_hbm,
     o_ref,
     span_ref,
-    span_sem,
-    wide_ref,
+    key_ref,
+    value_ref,
+    q_tiled,
+    kv_ref,
     held,
     top_ref,
     sum_ref,
     acc_ref,
+    load_sem,
     send_up,
     send_down,
     send_across,
     send_far,
     recv_sem,
 ):
-    rows, width = q_ref.shape
-    kv_rows = kv_ref.shape[0]
-    pair = kv_ref.shape[1] // 2
-    span = kv_rows // 2
-    chunk = kv_rows // CHUNKS
-    tiles = rows // TILE
+    tokens, groups, group_heads, width = q_hbm.shape
+    q_ref = q_tiled.reshape(groups * tokens * group_heads, width)
+    out_ref = o_ref.reshape(groups * tokens * group_heads, width)
+    rows = tokens * group_heads
+    span = tokens // 2
+    chunk = kv_ref.shape[0] // CHUNKS
+    tile = rows // 2
     factor = math.log2(math.e) / math.sqrt(width)
     outer = lax.axis_index("outer")
     inner = lax.axis_index("inner")
     far_halves = n_inner == 2 and n_outer > 2
     last = n_outer - 1
 
-    spans = pltpu.make_async_copy(span_hbm, span_ref, span_sem)
-    spans.start()
+    loads = [
+        pltpu.make_async_copy(key_hbm, key_ref, load_sem.at[0]),
+        pltpu.make_async_copy(value_hbm, value_ref, load_sem.at[1]),
+        pltpu.make_async_copy(span_hbm, span_ref, load_sem.at[2]),
+    ]
+    for group in range(groups):
+        loads.append(
+            pltpu.make_async_copy(q_hbm.at[:, group], q_tiled.at[group], load_sem.at[3 + group])
+        )
+    for load in loads:
+        load.start()
 
     barrier = pltpu.get_barrier_semaphore()
 
@@ -63,6 +77,14 @@
     for step in range(1, n_inner):
         peer = lax.rem(inner + step, n_inner)
         pl.semaphore_signal(barrier, inc=1, device_id={"inner": peer}, device_id_type=MESH)
+
+    loads[0].wait()
+    loads[1].wait()
+    for group in range(groups):
+        every = pl.ds(group, tokens, stride=groups)
+        here_rows = pl.ds(group * tokens, tokens)
+        kv_ref[here_rows, :width] = key_ref[every, :]
+        kv_ref[here_rows, width:] = value_ref[every, :]
 
     ends = jnp.minimum(outer, 1) + jnp.minimum(n_outer - 1 - outer, 1)
     pl.semaphore_wait(barrier, n_inner - 1 + ends)
@@ -154,49 +176,46 @@
     for part in range(CHUNKS):
         pass_on(kv_ref, outer, part, lambda copy: copy.start())
 
-    spans.wait()
-
-    row_head = lax.rem(lax.broadcasted_iota(jnp.int32, (TILE, width), 0), heads)
-    first_head = row_head < heads // 2
-    keep_first = jnp.where(first_head, 1.0, 0.0).astype(q_ref.dtype)
-    keep_second = jnp.where(first_head, 0.0, 1.0).astype(q_ref.dtype)
+    for load in loads[2:]:
+        load.wait()
+
     here = (outer * n_inner + inner) * 2
-    lane = lax.broadcasted_iota(jnp.int32, (TILE, kv_rows), 1)
-
-    def attend(block, value):
-        pv = jnp.dot(block.astype(jnp.bfloat16), value, preferred_element_type=jnp.float32)
-        return jnp.where(first_head, pv[:, :width], pv[:, width:])
-
-    def scores_of(wide, key):
+    lane = lax.broadcasted_iota(jnp.int32, (tile, tokens), 1)
+    tiles = [(group, block) for group in range(groups) for block in range(2)]
+
+    def at(index):
+        return pl.ds(index * tile, tile)
+
+    def scores_of(index, place):
+        group = tiles[index][0]
         return lax.dot_general(
-            wide, key, (((1,), (1,)), ((), ())), preferred_element_type=jnp.float32
-        )
-
-    def at(index):
-        return pl.ds(index * TILE, TILE)
-
-    def own_scores(index):
-        query = q_ref[at(index), :]
-        wide = jnp.concatenate([query * keep_first, query * keep_second], axis=1)
-        wide_ref[at(index), :] = wide
-        return scores_of(wide, kv_ref[:, :pair])
+            q_ref[at(index), :],
+            place[pl.ds(group * tokens, tokens), :width],
+            (((1,), (1,)), ((), ())),
+            preferred_element_type=jnp.float32,
+        )
+
+    def attend(index, weights, place):
+        group = tiles[index][0]
+        return jnp.dot(
+            weights.astype(jnp.bfloat16),
+            place[pl.ds(group * tokens, tokens), width:],
+            preferred_element_type=jnp.float32,
+        )
 
     def visit_own():
-        row = lax.broadcasted_iota(jnp.int32, (TILE, kv_rows), 0)
+        row = lax.broadcasted_iota(jnp.int32, (tile, tokens), 0)
         anchor = jnp.where(lane < span, span_ref[here], span_ref[here + 1])
-        ahead = anchor * span + lax.rem(lane, span) - row // heads
-        scores = own_scores(0)
-        for index in range(tiles):
-            following = own_scores(index + 1) if index + 1 < tiles else None
-            q_block = index // (tiles // 2)
-            q_offset = (index - q_block * (tiles // 2)) * TILE // heads
-            allowed = ahead <= span_ref[here + q_block] * span + q_offset
-            scores = jnp.where(allowed, scores, MASKED)
+        ahead = anchor * span + lax.rem(lane, span) - row // group_heads
+        scores = scores_of(0, kv_ref)
+        for index, (group, block) in enumerate(tiles):
+            following = scores_of(index + 1, kv_ref) if index + 1 < len(tiles) else None
+            scores = jnp.where(ahead <= span_ref[here + block] * span, scores, MASKED)
             top = jnp.max(scores, axis=1, keepdims=True)
             weights = jnp.exp2((scores - top) * factor)
-            top_ref[at(index), :] = jnp.broadcast_to(top, (TILE, width))
+            top_ref[at(index), :] = jnp.broadcast_to(top, (tile, width))
             sum_ref[at(index), :] = weights[:, :width] + weights[:, width:]
-            acc_ref[at(index), :] = attend(weights, kv_ref[:, pair:])
+            acc_ref[at(index), :] = attend(index, weights, kv_ref)
             scores = following
 
     visit_own()
@@ -209,16 +228,14 @@
         def settle_sum(index, rescale, added):
             acc_ref[at(index), :] = acc_ref[at(index), :] * rescale + added
 
-        scores = scores_of(wide_ref[at(0), :], place[:, :pair])
+        scores = scores_of(0, place)
         waiting = None
-        for index in range(tiles):
-            following = None
-            if index + 1 < tiles:
-                following = scores_of(wide_ref[at(index + 1), :], place[:, :pair])
-            q_anchor = span_ref[here + index // (tiles // 2)]
+        for index, (group, block) in enumerate(tiles):
+            following = scores_of(index + 1, place) if index + 1 < len(tiles) else None
+            q_anchor = span_ref[here + block]
             bias = [jnp.where(anchor < q_anchor, 0.0, MASKED) for anchor in anchors]
-            left = scores[:, :width] + bias[0]
-            right = scores[:, width:] + bias[1]
+            left = scores[:, :span] + bias[0]
+            right = scores[:, span:] + bias[1]
             old = top_ref[at(index), :]
             top = jnp.maximum(old, jnp.max(jnp.maximum(left, right), axis=1, keepdims=True))
             rescale = jnp.exp2((old - top) * factor)
@@ -226,8 +243,7 @@
             right = jnp.exp2((right - top) * factor)
             top_ref[at(index), :] = top
             sum_ref[at(index), :] = sum_ref[at(index), :] * rescale + (left + right)
-            weights = jnp.concatenate([left, right], axis=1)
-            added = attend(weights, place[:, pair:])
+            added = attend(index, jnp.concatenate([left, right], axis=1), place)
             if waiting is not None:
                 settle_sum(*waiting)
             waiting = (index, rescale, added)
@@ -303,9 +319,9 @@
     lax.fori_loop(1, n_outer + 1, line_step, 0)
     visit_sides(n_outer - 1, True)
 
-    for index in range(tiles):
+    for index in range(len(tiles)):
         total = jnp.sum(sum_ref[at(index), :], axis=1, keepdims=True)
-        o_ref[at(index), :] = (acc_ref[at(index), :] / total).astype(o_ref.dtype)
+        out_ref[at(index), :] = (acc_ref[at(index), :] / total).astype(o_ref.dtype)
 
     def settle(src_outer, carry):
         for part in range(CHUNKS):
@@ -319,30 +335,45 @@
                 far_on(end, part, lambda copy: copy.wait_send())
 
 
+def spread(o_ref, out_hbm, sem):
+    copies = [
+        pltpu.make_async_copy(o_ref.at[group], out_hbm.at[:, group], sem.at[group])
+        for group in range(o_ref.shape[0])
+    ]
+    for copy in copies:
+        copy.start()
+    for copy in copies:
+        copy.wait()
+
+
 def solution(mesh):
     n_outer, n_inner = mesh.shape["outer"], mesh.shape["inner"]
 
     def body(query, key, value, span_order):
-        kv_rows, groups, width = key.shape
+        tokens, groups, width = key.shape
         heads = query.shape[1]
-        rows = query.shape[0] * heads
-        kv = jnp.concatenate(
-            [key.reshape(kv_rows, groups * width), value.reshape(kv_rows, groups * width)], axis=1
-        )
+        group_heads = heads // groups
+        rows = tokens * heads
+        by_group = (groups, tokens, group_heads, width)
+        kv_shape = (groups * tokens, 2 * width)
         vmem = pl.BlockSpec(memory_space=pltpu.VMEM)
+        hbm = pl.BlockSpec(memory_space=pltpu.HBM)
         out = pl.pallas_call(
             functools.partial(kernel, n_outer, n_inner, heads),
-            out_shape=jax.ShapeDtypeStruct((rows, width), jnp.bfloat16),
-            in_specs=[pl.BlockSpec(memory_space=pltpu.HBM), vmem, vmem],
+            out_shape=jax.ShapeDtypeStruct(by_group, jnp.bfloat16),
+            in_specs=[hbm] * 4,
             out_specs=vmem,
             scratch_shapes=[
                 pltpu.SMEM(span_order.shape, jnp.int32),
-                pltpu.SemaphoreType.DMA,
-                pltpu.VMEM((rows, groups * width), jnp.bfloat16),
-                pltpu.VMEM((n_outer, n_inner) + kv.shape, jnp.bfloat16),
+                pltpu.VMEM((groups * tokens, width), jnp.bfloat16),
+                pltpu.VMEM((groups * tokens, width), jnp.bfloat16),
+                pltpu.VMEM(by_group, jnp.bfloat16),
+                pltpu.VMEM(kv_shape, jnp.bfloat16),
+                pltpu.VMEM((n_outer, n_inner) + kv_shape, jnp.bfloat16),
                 pltpu.VMEM((rows, width), jnp.float32),
                 pltpu.VMEM((rows, width), jnp.float32),
                 pltpu.VMEM((rows, width), jnp.float32),
+                pltpu.SemaphoreType.DMA((3 + groups,)),
                 pltpu.SemaphoreType.DMA((n_outer, CHUNKS)),
                 pltpu.SemaphoreType.DMA((n_outer, CHUNKS)),
                 pltpu.SemaphoreType.DMA((n_outer, CHUNKS, max(n_inner - 1, 1))),
@@ -350,9 +381,22 @@
                 pltpu.SemaphoreType.DMA((n_outer, n_inner, CHUNKS)),
             ],
             compiler_params=pltpu.CompilerParams(
-                collective_id=0, has_side_effects=True, vmem_limit_bytes=48 * 1024 * 1024
+                collective_id=0, has_side_effects=True, vmem_limit_bytes=VMEM_LIMIT
             ),
-        )(span_order, query.reshape(rows, width), kv)
+        )(
+            pltpu.with_memory_space_constraint(span_order, pltpu.HBM),
+            pltpu.with_memory_space_constraint(query.reshape(tokens, groups, group_heads, width), pltpu.HBM),
+            pltpu.with_memory_space_constraint(key.reshape(groups * tokens, width), pltpu.HBM),
+            pltpu.with_memory_space_constraint(value.reshape(groups * tokens, width), pltpu.HBM),
+        )
+        out = pl.pallas_call(
+            spread,
+            out_shape=jax.ShapeDtypeStruct((tokens, groups, group_heads, width), jnp.bfloat16),
+            in_specs=[vmem],
+            out_specs=hbm,
+            scratch_shapes=[pltpu.SemaphoreType.DMA((groups,))],
+            compiler_params=pltpu.CompilerParams(vmem_limit_bytes=1024 * 1024),
+        )(out)
         return out.reshape(query.shape)
 
     placed = P(("outer", "inner"), "head", None)

time: 32.1 us -> 30.2 us (0.941)
  local copies, waits for them, and re-layouts: 2.5 us -> 0 us
  Pallas kernels: 29.4 us -> 30.1 us
    unnamed x5 -> x0, local copies, waits for them, and re-layouts: 1.44 us -> none
    reshape x1 -> x0, local copies, waits for them, and re-layouts: 1.06 us -> none  [body(): value.reshape(kv_rows, groups * width)]
    pallas_call x0 -> x1, Pallas kernels: none -> 0.81 us  [body(): pl.pallas_call(spread, out_shape=jax.ShapeDtypeStruct((tokens, groups, gr...]
where the time goes in v2:
time: 30.2 us; the launch traced here: 30.1 us
  Pallas kernels  30.1 us (100%)
    pallas_call x1, Pallas kernels, body(): pl.pallas_call(functools.partial(kernel, n_outer, n_inner, heads), out_sh...  29.2 us
    pallas_call x1, Pallas kernels, body(): pl.pallas_call(spread, out_shape=jax.ShapeDtypeStruct((tokens, groups, gr...  0.81 us

profile of v2, /device:TPU:0, one launch (start us, length us, event | category | flops | bytes accessed | tf_op | source)
XLA Modules:
  0.0 30.1 jit_solution(3357179290260855946)
XLA Ops:
  0.0 29.2 %shard_map.46.o_ref = bf16[2,256,4,128]{3,2,1,0:T(4,128)(2,1)S(1)} custom-call(s32[16]{0:T(128)} %span_hbm.1, bf16[256,2,4,128]{3,2,1,0:T(4,128)(2,1)} %bitcast.4, bf16[512,128]{1,0:T(8,128)(2,1)} %bitcast.5, bf16[512,128]{1,0:T(8,128)(2,1)} %bitcast.6), custom_call_target="tpu_custom_call" | custom-call | tf_op jit(solution)/shard_map/pallas_call | solution.py:361
  29.3 0.8 %shard_map.47 = bf16[256,2,4,128]{3,2,1,0:T(4,128)(2,1)} custom-call(bf16[2,256,4,128]{3,2,1,0:T(4,128)(2,1)S(1)} %shard_map.46.o_ref), custom_call_target="tpu_custom_call" | custom-call | tf_op jit(solution)/shard_map/pallas_call | solution.py:392

commit v3 on v2

v3 whole, which is shorter than its diff:
```python
import functools
import math

import jax
import jax.numpy as jnp
from jax import lax
from jax.experimental import pallas as pl
from jax.experimental.pallas import tpu as pltpu
from jax.sharding import PartitionSpec as P

MESH = pl.DeviceIdType.MESH
MASKED = -1e30
VMEM_LIMIT = 48 * 1024 * 1024
CHUNKS = 4


def kernel(
    n_outer,
    n_inner,
    heads,
    span_hbm,
    q_hbm,
    key_hbm,
    value_hbm,
    o_ref,
    span_ref,
    key_ref,
    value_ref,
    q_tiled,
    q_ref,
    kv_ref,
    held,
    top_ref,
    sum_ref,
    acc_ref,
    load_sem,
    send_sem,
    recv_sem,
):
    tokens, groups, group_heads, width = q_hbm.shape
    q_rows = q_tiled.reshape(groups * tokens * group_heads, width)
    out_ref = o_ref.reshape(groups * tokens * group_heads, width)
    rows = tokens * group_heads
    span = tokens // 2
    chunk = kv_ref.shape[0] // CHUNKS
    tile = rows // 2
    factor = math.log2(math.e) / math.sqrt(width)
    outer = lax.axis_index("outer")
    inner = lax.axis_index("inner")
    far_halves = n_inner == 2 and n_outer > 2
    last = n_outer - 1

    loads = [
        pltpu.make_async_copy(key_hbm, key_ref, load_sem.at[0]),
        pltpu.make_async_copy(value_hbm, value_ref, load_sem.at[1]),
        pltpu.make_async_copy(span_hbm, span_ref, load_sem.at[2]),
    ]
    for group in range(groups):
        loads.append(
            pltpu.make_async_copy(q_hbm.at[:, group], q_tiled.at[group], load_sem.at[3])
        )
    for load in loads:
        load.start()

    barrier = pltpu.get_barrier_semaphore()

    @pl.when(outer > 0)
    def _():
        pl.semaphore_signal(barrier, inc=1, device_id={"outer": outer - 1}, device_id_type=MESH)

    @pl.when(outer < n_outer - 1)
    def _():
        pl.semaphore_signal(barrier, inc=1, device_id={"outer": outer + 1}, device_id_type=MESH)

    for step in range(1, n_inner):
        peer = lax.rem(inner + step, n_inner)
        pl.semaphore_signal(barrier, inc=1, device_id={"inner": peer}, device_id_type=MESH)

    loads[0].wait()
    loads[1].wait()
    for group in range(groups):
        every = pl.ds(group, tokens, stride=groups)
        here_rows = pl.ds(group * tokens, tokens)
        kv_ref[here_rows, :width] = key_ref[every, :]
        kv_ref[here_rows, width:] = value_ref[every, :]

    ends = jnp.minimum(outer, 1) + jnp.minimum(n_outer - 1 - outer, 1)
    pl.semaphore_wait(barrier, n_inner - 1 + ends)

    def copy_of(source, src_outer, src_inner, part, target):
        return pltpu.make_async_remote_copy(
            src_ref=source.at[pl.ds(part * chunk, chunk)],
            dst_ref=held.at[src_outer, src_inner, pl.ds(part * chunk, chunk)],
            send_sem=send_sem,
            recv_sem=recv_sem.at[src_outer, src_inner, part],
            device_id=target,
            device_id_type=MESH,
        )

    def up(source, src_outer, part):
        return copy_of(source, src_outer, inner, part, {"outer": outer + 1})

    def down(source, src_outer, part):
        return copy_of(source, src_outer, inner, part, {"outer": outer - 1})

    def across(source, src_outer, part, step):
        peer = lax.rem(inner + step, n_inner)
        return copy_of(source, src_outer, inner, part, {"inner": peer})

    def is_far(src_outer):
        return jnp.logical_or(src_outer == 0, src_outer == last)

    def crosses(src_outer, part):
        if not far_halves or part < CHUNKS // 2:
            return jnp.bool_(True)
        return jnp.logical_or(src_outer == outer, jnp.logical_not(is_far(src_outer)))

    def pass_on(source, src_outer, part, act):
        going_up = jnp.logical_and(src_outer <= outer, outer < last)
        going_down = jnp.logical_and(src_outer >= outer, outer > 0)
        upper = outer >= n_outer // 2

        @pl.when(jnp.logical_and(going_up, upper))
        def _():
            act(up(source, src_outer, part))

        @pl.when(going_down)
        def _():
            act(down(source, src_outer, part))

        @pl.when(crosses(src_outer, part))
        def _():
            for step in range(1, n_inner):
                act(across(source, src_outer, part, step))

        @pl.when(jnp.logical_and(going_up, jnp.logical_not(upper)))
        def _():
            act(up(source, src_outer, part))

    def far_on(src_outer, part, act):
        other = n_inner - 1 - inner
        source = held.at[src_outer, other]

        @pl.when(jnp.logical_and(src_outer == 0, outer < last))
        def _():
            act(copy_of(source, 0, other, part, {"outer": outer + 1}))

        @pl.when(jnp.logical_and(src_outer == last, outer > 0))
        def _():
            act(copy_of(source, last, other, part, {"outer": outer - 1}))

    def arrived(src_outer, src_inner, part):
        place = held.at[src_outer, src_inner, pl.ds(part * chunk, chunk)]
        pltpu.make_async_remote_copy(
            src_ref=place,
            dst_ref=place,
            send_sem=recv_sem.at[src_outer, src_inner, part],
            recv_sem=recv_sem.at[src_outer, src_inner, part],
            device_id={"inner": lax.rem(inner + 1, n_inner)},
            device_id_type=MESH,
        ).wait_recv()

    for part in range(CHUNKS):
        pass_on(kv_ref, outer, part, lambda copy: copy.start())

    loads[2].wait()
    pltpu.make_async_copy(q_tiled, q_tiled, load_sem.at[3]).wait()

    here = (outer * n_inner + inner) * 2
    lane = lax.broadcasted_iota(jnp.int32, (tile, tokens), 1)
    tiles = [(group, block) for group in range(groups) for block in range(2)]

    def at(group, block):
        return pl.ds((group * 2 + block) * tile, tile)

    column = lax.broadcasted_iota(jnp.int32, (tile, width), 1)
    for group, block in tiles:
        q_ref[at(group, block), :width] = q_rows[at(group, block), :]
        q_ref[at(group, block), width:] = jnp.where(column == block, 1.0, 0.0).astype(q_ref.dtype)

    def biases(base):
        column = lax.broadcasted_iota(jnp.int32, (span, width), 1)
        halves = []
        for half in range(2):
            bias = [
                jnp.where(span_ref[base + half] < span_ref[here + block], 0.0, MASKED)
                for block in range(2)
            ]
            halves.append(jnp.where(column == 0, bias[0], jnp.where(column == 1, bias[1], 0.0)))
        return jnp.concatenate(halves, axis=0).astype(kv_ref.dtype)

    def scores_of(group, block, place, bias=None):
        keys = place[pl.ds(group * tokens, tokens), :width]
        queries = q_ref[at(group, block), :width]
        if bias is not None:
            keys = jnp.concatenate([keys, bias], axis=1)
            queries = q_ref[at(group, block), :]
        return lax.dot_general(
            queries, keys, (((1,), (1,)), ((), ())), preferred_element_type=jnp.float32
        )

    def attend(group, weights, place):
        return jnp.dot(
            weights.astype(jnp.bfloat16),
            place[pl.ds(group * tokens, tokens), width:],
            preferred_element_type=jnp.float32,
        )

    def visit_own():
        row = lax.broadcasted_iota(jnp.int32, (tile, tokens), 0)
        anchor = jnp.where(lane < span, span_ref[here], span_ref[here + 1])
        ahead = anchor * span + lax.rem(lane, span) - row // group_heads
        scores = scores_of(*tiles[0], kv_ref)
        for index, (group, block) in enumerate(tiles):
            following = None
            if index + 1 < len(tiles):
                following = scores_of(*tiles[index + 1], kv_ref)
            some = at(group, block)
            scores = jnp.where(ahead <= span_ref[here + block] * span, scores, MASKED)
            top = jnp.max(scores, axis=1, keepdims=True)
            weights = jnp.exp2((scores - top) * factor)
            top_ref[some, :] = jnp.broadcast_to(top, (tile, width))
            sum_ref[some, :] = weights[:, :width] + weights[:, width:]
            acc_ref[some, :] = attend(group, weights, kv_ref)
            scores = following

    visit_own()

    def visit(src_outer, src_inner, group, final=False):
        bias = biases((src_outer * n_inner + src_inner) * 2)
        place = held.at[src_outer, src_inner]

        def settle_sum(some, rescale, added, sums):
            acc = acc_ref[some, :] * rescale + added
            if final:
                total = jnp.sum(sums, axis=1, keepdims=True)
                out_ref[some, :] = (acc / total).astype(o_ref.dtype)
            else:
                acc_ref[some, :] = acc

        scores = scores_of(group, 0, place, bias)
        waiting = None
        for block in range(2):
            following = scores_of(group, 1, place, bias) if block == 0 else None
            some = at(group, block)
            left, right = scores[:, :span], scores[:, span:]
            old = top_ref[some, :]
            top = jnp.maximum(old, jnp.max(jnp.maximum(left, right), axis=1, keepdims=True))
            rescale = jnp.exp2((old - top) * factor)
            left = jnp.exp2((left - top) * factor)
            right = jnp.exp2((right - top) * factor)
            sums = sum_ref[some, :] * rescale + (left + right)
            if not final:
                top_ref[some, :] = top
                sum_ref[some, :] = sums
            added = attend(group, jnp.concatenate([left, right], axis=1), place)
            if waiting is not None:
                settle_sum(*waiting)
            waiting = (some, rescale, added, sums)
            scores = following
        settle_sum(*waiting)

    end_outer = jnp.where(outer < n_outer // 2, last, 0)
    first_half, second_half = range(CHUNKS // 2), range(CHUNKS // 2, CHUNKS)
    parts_of = [first_half, second_half]

    def take(step, parts):
        for part in parts:
            for side in (1, -1):
                src_outer = outer + side * step

                @pl.when(jnp.logical_and(src_outer >= 0, src_outer < n_outer))
                def _():
                    arrived(src_outer, inner, part)
                    pass_on(
                        held.at[src_outer, inner], src_outer, part, lambda copy: copy.start()
                    )

    def take_far(step):
        for side, end in ((1, last), (-1, 0)):

            @pl.when(outer + side * step == end + side)
            def _():
                for part in second_half:
                    arrived(end, n_inner - 1 - inner, part)
                    far_on(end, part, lambda copy: copy.start())

    def sides(distance, act):
        def one(side, carry):
            src_outer = outer + (1 - 2 * side) * distance

            @pl.when(
                jnp.logical_and(
                    jnp.logical_and(src_outer >= 0, src_outer < n_outer),
                    jnp.logical_and(distance >= 0, jnp.logical_or(distance > 0, side == 0)),
                )
            )
            def _():
                act(src_outer)

            return carry

        lax.fori_loop(0, 2, one, 0)

    def visit_others(src_outer):
        def of_inner(step, carry):
            src_inner = lax.rem(inner + step, n_inner)
            for group in range(groups):
                for part in parts_of[group]:
                    if far_halves and group > 0:

                        @pl.when(jnp.logical_not(is_far(src_outer)))
                        def _():
                            arrived(src_outer, src_inner, part)
                    else:
                        arrived(src_outer, src_inner, part)
                visit(src_outer, src_inner, group)
            return carry

        until = jnp.where(src_outer == end_outer, n_inner - 1, n_inner)
        lax.fori_loop(1, until, of_inner, 0)

    def line_step(step, carry):
        take(step, first_half)
        if far_halves:
            take_far(step)
        sides(step, lambda src_outer: visit(src_outer, inner, 0))
        sides(step - 2 + jnp.where(is_far(outer), 1, 0), visit_others)
        take(step, second_half)
        sides(step, lambda src_outer: visit(src_outer, inner, 1))
        return carry

    lax.fori_loop(1, n_outer, line_step, 0)
    if n_inner > 2:
        sides(jnp.abs(end_outer - outer), visit_others)

    end_inner = lax.rem(inner + n_inner - 1, n_inner)
    for group in range(groups):
        for part in parts_of[group]:
            if far_halves and group > 0:

                @pl.when(is_far(outer))
                def _():
                    arrived(end_outer, end_inner, part)
            else:
                arrived(end_outer, end_inner, part)
        visit(end_outer, end_inner, group, final=True)

    def settle(src_outer, carry):
        for part in range(CHUNKS):
            pass_on(kv_ref, src_outer, part, lambda copy: copy.wait_send())
        return carry

    lax.fori_loop(0, n_outer, settle, 0)
    if far_halves:
        for part in second_half:
            for end in (0, last):
                far_on(end, part, lambda copy: copy.wait_send())


def spread(o_ref, out_hbm, sem):
    copies = [
        pltpu.make_async_copy(o_ref.at[group], out_hbm.at[:, group], sem.at[group])
        for group in range(o_ref.shape[0])
    ]
    for copy in copies:
        copy.start()
    for copy in copies:
        copy.wait()


def solution(mesh):
    n_outer, n_inner = mesh.shape["outer"], mesh.shape["inner"]

    def body(query, key, value, span_order):
        tokens, groups, width = key.shape
        heads = query.shape[1]
        group_heads = heads // groups
        rows = tokens * heads
        by_group = (groups, tokens, group_heads, width)
        kv_shape = (groups * tokens, 2 * width)
        vmem = pl.BlockSpec(memory_space=pltpu.VMEM)
        hbm = pl.BlockSpec(memory_space=pltpu.HBM)
        out = pl.pallas_call(
            functools.partial(kernel, n_outer, n_inner, heads),
            out_shape=jax.ShapeDtypeStruct(by_group, jnp.bfloat16),
            in_specs=[hbm] * 4,
            out_specs=vmem,
            scratch_shapes=[
                pltpu.SMEM(span_order.shape, jnp.int32),
                pltpu.VMEM((groups * tokens, width), jnp.bfloat16),
                pltpu.VMEM((groups * tokens, width), jnp.bfloat16),
                pltpu.VMEM(by_group, jnp.bfloat16),
                pltpu.VMEM((rows, 2 * width), jnp.bfloat16),
                pltpu.VMEM(kv_shape, jnp.bfloat16),
                pltpu.VMEM((n_outer, n_inner) + kv_shape, jnp.bfloat16),
                pltpu.VMEM((rows, width), jnp.float32),
                pltpu.VMEM((rows, width), jnp.float32),
                pltpu.VMEM((rows, width), jnp.float32),
                pltpu.SemaphoreType.DMA((4,)),
                pltpu.SemaphoreType.DMA,
                pltpu.SemaphoreType.DMA((n_outer, n_inner, CHUNKS)),
            ],
            compiler_params=pltpu.CompilerParams(
                collective_id=0, has_side_effects=True, vmem_limit_bytes=VMEM_LIMIT
            ),
        )(
            pltpu.with_memory_space_constraint(span_order, pltpu.HBM),
            pltpu.with_memory_space_constraint(query.reshape(tokens, groups, group_heads, width), pltpu.HBM),
            pltpu.with_memory_space_constraint(key.reshape(groups * tokens, width), pltpu.HBM),
            pltpu.with_memory_space_constraint(value.reshape(groups * tokens, width), pltpu.HBM),
        )
        out = pl.pallas_call(
            spread,
            out_shape=jax.ShapeDtypeStruct((tokens, groups, group_heads, width), jnp.bfloat16),
            in_specs=[vmem],
            out_specs=hbm,
            scratch_shapes=[pltpu.SemaphoreType.DMA((groups,))],
            compiler_params=pltpu.CompilerParams(vmem_limit_bytes=1024 * 1024),
        )(out)
        return out.reshape(query.shape)

    placed = P(("outer", "inner"), "head", None)
    return jax.shard_map(
        body,
        mesh=mesh,
        in_specs=(placed, placed, placed, P()),
        out_specs=placed,
        check_vma=False,
    )
```

time: 30.2 us -> 27.6 us (0.914)
  Pallas kernels: 30.1 us -> 27.4 us
    pallas_call x1, Pallas kernels: 29.2 us -> 26.6 us  [body(): pl.pallas_call(functools.partial(kernel, n_outer, n_inner, heads), out_sh...]
where the time goes in v3:
time: 27.6 us; the launch traced here: 27.4 us
  Pallas kernels  27.4 us (99%)
    pallas_call x1, Pallas kernels, body(): pl.pallas_call(functools.partial(kernel, n_outer, n_inner, heads), out_sh...  26.6 us
    pallas_call x1, Pallas kernels, body(): pl.pallas_call(spread, out_shape=jax.ShapeDtypeStruct((tokens, groups, gr...  0.81 us

profile of v3, /device:TPU:0, one launch (start us, length us, event | category | flops | bytes accessed | tf_op | source)
XLA Modules:
  0.0 27.4 jit_solution(4597383866104120803)
XLA Ops:
  0.0 26.6 %shard_map.46.o_ref = bf16[2,256,4,128]{3,2,1,0:T(4,128)(2,1)S(1)} custom-call(s32[16]{0:T(128)} %span_hbm.1, bf16[256,2,4,128]{3,2,1,0:T(4,128)(2,1)} %bitcast.4, bf16[512,128]{1,0:T(8,128)(2,1)} %bitcast.5, bf16[512,128]{1,0:T(8,128)(2,1)} %bitcast.6), custom_call_target="tpu_custom_call" | custom-call | tf_op jit(solution)/shard_map/pallas_call | solution.py:384
  26.6 0.8 %shard_map.47 = bf16[256,2,4,128]{3,2,1,0:T(4,128)(2,1)} custom-call(bf16[2,256,4,128]{3,2,1,0:T(4,128)(2,1)S(1)} %shard_map.46.o_ref), custom_call_target="tpu_custom_call" | custom-call | tf_op jit(solution)/shard_map/pallas_call | solution.py:413

commit v4 on v3

--- a/solution.py
+++ b/solution.py
@@ -226,7 +226,7 @@
 
     visit_own()
 
-    def visit(src_outer, src_inner, group, final=False):
+    def visit(src_outer, src_inner, visited, final=False):
         bias = biases((src_outer * n_inner + src_inner) * 2)
         place = held.at[src_outer, src_inner]
 
@@ -238,10 +238,12 @@
             else:
                 acc_ref[some, :] = acc
 
-        scores = scores_of(group, 0, place, bias)
+        scores = scores_of(*visited[0], place, bias)
         waiting = None
-        for block in range(2):
-            following = scores_of(group, 1, place, bias) if block == 0 else None
+        for index, (group, block) in enumerate(visited):
+            following = None
+            if index + 1 < len(visited):
+                following = scores_of(*visited[index + 1], place, bias)
             some = at(group, block)
             left, right = scores[:, :span], scores[:, span:]
             old = top_ref[some, :]
@@ -263,6 +265,7 @@
     end_outer = jnp.where(outer < n_outer // 2, last, 0)
     first_half, second_half = range(CHUNKS // 2), range(CHUNKS // 2, CHUNKS)
     parts_of = [first_half, second_half]
+    tiles_of = [[(group, block) for block in range(2)] for group in range(groups)]
 
     def take(step, parts):
         for part in parts:
@@ -314,7 +317,7 @@
                             arrived(src_outer, src_inner, part)
                     else:
                         arrived(src_outer, src_inner, part)
-                visit(src_outer, src_inner, group)
+                visit(src_outer, src_inner, tiles_of[group])
             return carry
 
         until = jnp.where(src_outer == end_outer, n_inner - 1, n_inner)
@@ -324,27 +327,15 @@
         take(step, first_half)
         if far_halves:
             take_far(step)
-        sides(step, lambda src_outer: visit(src_outer, inner, 0))
+        sides(step, lambda src_outer: visit(src_outer, inner, tiles_of[0]))
         sides(step - 2 + jnp.where(is_far(outer), 1, 0), visit_others)
         take(step, second_half)
-        sides(step, lambda src_outer: visit(src_outer, inner, 1))
+        sides(step, lambda src_outer: visit(src_outer, inner, tiles_of[1]))
         return carry
 
     lax.fori_loop(1, n_outer, line_step, 0)
     if n_inner > 2:
         sides(jnp.abs(end_outer - outer), visit_others)
-
-    end_inner = lax.rem(inner + n_inner - 1, n_inner)
-    for group in range(groups):
-        for part in parts_of[group]:
-            if far_halves and group > 0:
-
-                @pl.when(is_far(outer))
-                def _():
-                    arrived(end_outer, end_inner, part)
-            else:
-                arrived(end_outer, end_inner, part)
-        visit(end_outer, end_inner, group, final=True)
 
     def settle(src_outer, carry):
         for part in range(CHUNKS):
@@ -356,6 +347,17 @@
         for part in second_half:
             for end in (0, last):
                 far_on(end, part, lambda copy: copy.wait_send())
+
+    end_inner = lax.rem(inner + n_inner - 1, n_inner)
+    for part in range(CHUNKS):
+        if far_halves and part >= CHUNKS // 2:
+
+            @pl.when(is_far(outer))
+            def _():
+                arrived(end_outer, end_inner, part)
+        else:
+            arrived(end_outer, end_inner, part)
+    visit(end_outer, end_inner, tiles, final=True)
 
 
 def spread(o_ref, out_hbm, sem):

time: 27.6 us -> 27.3 us (0.989)
  no operation moved by 1% of the time
where the time goes in v4:
time: 27.3 us; the launch traced here: 27.2 us
  Pallas kernels  27.2 us (100%)
    pallas_call x1, Pallas kernels, body(): pl.pallas_call(functools.partial(kernel, n_outer, n_inner, heads), out_sh...  26.4 us
    pallas_call x1, Pallas kernels, body(): pl.pallas_call(spread, out_shape=jax.ShapeDtypeStruct((tokens, groups, gr...  0.81 us

profile of v4, /device:TPU:0, one launch (start us, length us, event | category | flops | bytes accessed | tf_op | source)
XLA Modules:
  0.0 27.2 jit_solution(8884368889441018163)
XLA Ops:
  0.0 26.4 %shard_map.46.o_ref = bf16[2,256,4,128]{3,2,1,0:T(4,128)(2,1)S(1)} custom-call(s32[16]{0:T(128)} %span_hbm.1, bf16[256,2,4,128]{3,2,1,0:T(4,128)(2,1)} %bitcast.4, bf16[512,128]{1,0:T(8,128)(2,1)} %bitcast.5, bf16[512,128]{1,0:T(8,128)(2,1)} %bitcast.6), custom_call_target="tpu_custom_call" | custom-call | tf_op jit(solution)/shard_map/pallas_call | solution.py:386
  26.4 0.8 %shard_map.47 = bf16[256,2,4,128]{3,2,1,0:T(4,128)(2,1)} custom-call(bf16[2,256,4,128]{3,2,1,0:T(4,128)(2,1)S(1)} %shard_map.46.o_ref), custom_call_target="tpu_custom_call" | custom-call | tf_op jit(solution)/shard_map/pallas_call | solution.py:415

commit v5 on v4

--- a/solution.py
+++ b/solution.py
@@ -334,8 +334,12 @@
         return carry
 
     lax.fori_loop(1, n_outer, line_step, 0)
-    if n_inner > 2:
-        sides(jnp.abs(end_outer - outer), visit_others)
+    if n_inner > 2 or n_outer % 2 == 1:
+        end_distance = jnp.abs(end_outer - outer)
+
+        @pl.when(end_distance >= n_outer - 2)
+        def _():
+            sides(end_distance, visit_others)
 
     def settle(src_outer, carry):
         for part in range(CHUNKS):

time: 27.3 us -> 27.3 us (level)
  no operation moved by 1% of the time
where the time goes in v5:
time: 27.3 us; the launch traced here: 27.2 us
  Pallas kernels  27.2 us (100%)
    pallas_call x1, Pallas kernels, body(): pl.pallas_call(functools.partial(kernel, n_outer, n_inner, heads), out_sh...  26.4 us
    pallas_call x1, Pallas kernels, body(): pl.pallas_call(spread, out_shape=jax.ShapeDtypeStruct((tokens, groups, gr...  0.81 us

profile of v5, /device:TPU:0, one launch (start us, length us, event | category | flops | bytes accessed | tf_op | source)
XLA Modules:
  0.0 27.2 jit_solution(8884368889441018163)
XLA Ops:
  0.0 26.4 %shard_map.46.o_ref = bf16[2,256,4,128]{3,2,1,0:T(4,128)(2,1)S(1)} custom-call(s32[16]{0:T(128)} %span_hbm.1, bf16[256,2,4,128]{3,2,1,0:T(4,128)(2,1)} %bitcast.4, bf16[512,128]{1,0:T(8,128)(2,1)} %bitcast.5, bf16[512,128]{1,0:T(8,128)(2,1)} %bitcast.6), custom_call_target="tpu_custom_call" | custom-call | tf_op jit(solution)/shard_map/pallas_call | solution.py:390
  26.4 0.8 %shard_map.47 = bf16[256,2,4,128]{3,2,1,0:T(4,128)(2,1)} custom-call(bf16[2,256,4,128]{3,2,1,0:T(4,128)(2,1)S(1)} %shard_map.46.o_ref), custom_call_target="tpu_custom_call" | custom-call | tf_op jit(solution)/shard_map/pallas_call | solution.py:419

commit v6 on v5

--- a/solution.py
+++ b/solution.py
@@ -48,6 +48,7 @@
     outer = lax.axis_index("outer")
     inner = lax.axis_index("inner")
     far_halves = n_inner == 2 and n_outer > 2
+    far_parts = range(CHUNKS // 2, CHUNKS)
     last = n_outer - 1
 
     loads = [
@@ -111,7 +112,7 @@
         return jnp.logical_or(src_outer == 0, src_outer == last)
 
     def crosses(src_outer, part):
-        if not far_halves or part < CHUNKS // 2:
+        if not far_halves or part not in far_parts:
             return jnp.bool_(True)
         return jnp.logical_or(src_outer == outer, jnp.logical_not(is_far(src_outer)))
 
@@ -226,9 +227,13 @@
 
     visit_own()
 
-    def visit(src_outer, src_inner, visited, final=False):
-        bias = biases((src_outer * n_inner + src_inner) * 2)
-        place = held.at[src_outer, src_inner]
+    def visit(blocks, visited, final=False):
+        bias = [biases((src_outer * n_inner + src_inner) * 2) for src_outer, src_inner in blocks]
+        places = [held.at[src_outer, src_inner] for src_outer, src_inner in blocks]
+
+        def all_scores(index):
+            scores = [scores_of(*visited[index], *place) for place in zip(places, bias)]
+            return [half for score in scores for half in (score[:, :span], score[:, span:])]
 
         def settle_sum(some, rescale, added, sums):
             acc = acc_ref[some, :] * rescale + added
@@ -238,24 +243,25 @@
             else:
                 acc_ref[some, :] = acc
 
-        scores = scores_of(*visited[0], place, bias)
+        scores = all_scores(0)
         waiting = None
         for index, (group, block) in enumerate(visited):
-            following = None
-            if index + 1 < len(visited):
-                following = scores_of(*visited[index + 1], place, bias)
+            following = all_scores(index + 1) if index + 1 < len(visited) else None
             some = at(group, block)
-            left, right = scores[:, :span], scores[:, span:]
             old = top_ref[some, :]
-            top = jnp.maximum(old, jnp.max(jnp.maximum(left, right), axis=1, keepdims=True))
+            top = functools.reduce(jnp.maximum, scores)
+            top = jnp.maximum(old, jnp.max(top, axis=1, keepdims=True))
             rescale = jnp.exp2((old - top) * factor)
-            left = jnp.exp2((left - top) * factor)
-            right = jnp.exp2((right - top) * factor)
-            sums = sum_ref[some, :] * rescale + (left + right)
+            weights = [jnp.exp2((score - top) * factor) for score in scores]
+            sums = sum_ref[some, :] * rescale + sum(weights[1:], weights[0])
             if not final:
                 top_ref[some, :] = top
                 sum_ref[some, :] = sums
-            added = attend(group, jnp.concatenate([left, right], axis=1), place)
+            added = [
+                attend(group, jnp.concatenate(weights[2 * k : 2 * k + 2], axis=1), place)
+                for k, place in enumerate(places)
+            ]
+            added = sum(added[1:], added[0])
             if waiting is not None:
                 settle_sum(*waiting)
             waiting = (some, rescale, added, sums)
@@ -284,7 +290,7 @@
 
             @pl.when(outer + side * step == end + side)
             def _():
-                for part in second_half:
+                for part in far_parts:
                     arrived(end, n_inner - 1 - inner, part)
                     far_on(end, part, lambda copy: copy.start())
 
@@ -310,27 +316,54 @@
             src_inner = lax.rem(inner + step, n_inner)
             for group in range(groups):
                 for part in parts_of[group]:
-                    if far_halves and group > 0:
+                    if far_halves and part in far_parts:
 
                         @pl.when(jnp.logical_not(is_far(src_outer)))
                         def _():
                             arrived(src_outer, src_inner, part)
                     else:
                         arrived(src_outer, src_inner, part)
-                visit(src_outer, src_inner, tiles_of[group])
+                visit([(src_outer, src_inner)], tiles_of[group])
             return carry
 
         until = jnp.where(src_outer == end_outer, n_inner - 1, n_inner)
         lax.fori_loop(1, until, of_inner, 0)
+
+    def pair_at_end(step, group):
+        away = jnp.where(outer == 0, 1, -1)
+        above, before = outer + away * step, outer + away * (step - 1)
+        for part in parts_of[group]:
+            if part in far_parts:
+
+                @pl.when(jnp.logical_not(is_far(before)))
+                def _():
+                    arrived(before, n_inner - 1 - inner, part)
+            else:
+                arrived(before, n_inner - 1 - inner, part)
+        visit([(above, inner), (before, n_inner - 1 - inner)], tiles_of[group])
+
+    def sides_at(step, group):
+        sides(step, lambda src_outer: visit([(src_outer, inner)], tiles_of[group]))
 
     def line_step(step, carry):
         take(step, first_half)
         if far_halves:
             take_far(step)
-        sides(step, lambda src_outer: visit(src_outer, inner, tiles_of[0]))
-        sides(step - 2 + jnp.where(is_far(outer), 1, 0), visit_others)
+            pl.when(is_far(outer))(lambda: pair_at_end(step, 0))
+
+            @pl.when(jnp.logical_not(is_far(outer)))
+            def _():
+                sides_at(step, 0)
+                sides(step - 2, visit_others)
+        else:
+            sides_at(step, 0)
+            sides(step - 2 + jnp.where(is_far(outer), 1, 0), visit_others)
         take(step, second_half)
-        sides(step, lambda src_outer: visit(src_outer, inner, tiles_of[1]))
+        if far_halves:
+            pl.when(is_far(outer))(lambda: pair_at_end(step, 1))
+            pl.when(jnp.logical_not(is_far(outer)))(lambda: sides_at(step, 1))
+        else:
+            sides_at(step, 1)
         return carry
 
     lax.fori_loop(1, n_outer, line_step, 0)
@@ -348,20 +381,20 @@
 
     lax.fori_loop(0, n_outer, settle, 0)
     if far_halves:
-        for part in second_half:
+        for part in far_parts:
             for end in (0, last):
                 far_on(end, part, lambda copy: copy.wait_send())
 
     end_inner = lax.rem(inner + n_inner - 1, n_inner)
     for part in range(CHUNKS):
-        if far_halves and part >= CHUNKS // 2:
+        if far_halves and part in far_parts:
 
             @pl.when(is_far(outer))
             def _():
                 arrived(end_outer, end_inner, part)
         else:
             arrived(end_outer, end_inner, part)
-    visit(end_outer, end_inner, tiles, final=True)
+    visit([(end_outer, end_inner)], tiles, final=True)
 
 
 def spread(o_ref, out_hbm, sem):

time: 27.3 us -> 27.1 us (level)
  no operation moved by 1% of the time
where the time goes in v6:
time: 27.1 us; the launch traced here: 27 us
  Pallas kernels  27 us (100%)
    pallas_call x1, Pallas kernels, body(): pl.pallas_call(functools.partial(kernel, n_outer, n_inner, heads), out_sh...  26.2 us
    pallas_call x1, Pallas kernels, body(): pl.pallas_call(spread, out_shape=jax.ShapeDtypeStruct((tokens, groups, gr...  0.81 us

profile of v6, /device:TPU:0, one launch (start us, length us, event | category | flops | bytes accessed | tf_op | source)
XLA Modules:
  0.0 27.0 jit_solution(16198127393078659617)
XLA Ops:
  0.0 26.2 %shard_map.46.o_ref = bf16[2,256,4,128]{3,2,1,0:T(4,128)(2,1)S(1)} custom-call(s32[16]{0:T(128)} %span_hbm.1, bf16[256,2,4,128]{3,2,1,0:T(4,128)(2,1)} %bitcast.4, bf16[512,128]{1,0:T(8,128)(2,1)} %bitcast.5, bf16[512,128]{1,0:T(8,128)(2,1)} %bitcast.6), custom_call_target="tpu_custom_call" | custom-call | tf_op jit(solution)/shard_map/pallas_call | solution.py:423
  26.2 0.8 %shard_map.47 = bf16[256,2,4,128]{3,2,1,0:T(4,128)(2,1)} custom-call(bf16[2,256,4,128]{3,2,1,0:T(4,128)(2,1)S(1)} %shard_map.46.o_ref), custom_call_target="tpu_custom_call" | custom-call | tf_op jit(solution)/shard_map/pallas_call | solution.py:452

commit v7 on v6

--- a/solution.py
+++ b/solution.py
@@ -12,6 +12,7 @@
 MASKED = -1e30
 VMEM_LIMIT = 48 * 1024 * 1024
 CHUNKS = 4
+PIECES = 8
 
 
 def kernel(
@@ -398,14 +399,14 @@
 
 
 def spread(o_ref, out_hbm, sem):
-    copies = [
-        pltpu.make_async_copy(o_ref.at[group], out_hbm.at[:, group], sem.at[group])
-        for group in range(o_ref.shape[0])
-    ]
-    for copy in copies:
-        copy.start()
-    for copy in copies:
-        copy.wait()
+    groups, tokens = o_ref.shape[:2]
+    some = tokens // PIECES
+    for first in range(0, tokens, some):
+        for group in range(groups):
+            pltpu.make_async_copy(
+                o_ref.at[group, pl.ds(first, some)], out_hbm.at[pl.ds(first, some), group], sem
+            ).start()
+    pltpu.make_async_copy(o_ref, o_ref, sem).wait()
 
 
 def solution(mesh):
@@ -454,7 +455,7 @@
             out_shape=jax.ShapeDtypeStruct((tokens, groups, group_heads, width), jnp.bfloat16),
             in_specs=[vmem],
             out_specs=hbm,
-            scratch_shapes=[pltpu.SemaphoreType.DMA((groups,))],
+            scratch_shapes=[pltpu.SemaphoreType.DMA],
             compiler_params=pltpu.CompilerParams(vmem_limit_bytes=1024 * 1024),
         )(out)
         return out.reshape(query.shape)

time: 27.1 us -> 27.1 us (level)
  no operation moved by 1% of the time
where the time goes in v7:
time: 27.1 us; the launch traced here: 27 us
  Pallas kernels  27 us (100%)
    pallas_call x1, Pallas kernels, body(): pl.pallas_call(functools.partial(kernel, n_outer, n_inner, heads), out_sh...  26.2 us
    pallas_call x1, Pallas kernels, body(): pl.pallas_call(spread, out_shape=jax.ShapeDtypeStruct((tokens, groups, gr...  0.78 us

profile of v7, /device:TPU:0, one launch (start us, length us, event | category | flops | bytes accessed | tf_op | source)
XLA Modules:
  0.0 27.0 jit_solution(2812464760814979987)
XLA Ops:
  0.0 26.2 %shard_map.46.o_ref = bf16[2,256,4,128]{3,2,1,0:T(4,128)(2,1)S(1)} custom-call(s32[16]{0:T(128)} %span_hbm.1, bf16[256,2,4,128]{3,2,1,0:T(4,128)(2,1)} %bitcast.4, bf16[512,128]{1,0:T(8,128)(2,1)} %bitcast.5, bf16[512,128]{1,0:T(8,128)(2,1)} %bitcast.6), custom_call_target="tpu_custom_call" | custom-call | tf_op jit(solution)/shard_map/pallas_call | solution.py:424
  26.2 0.8 %shard_map.47 = bf16[256,2,4,128]{3,2,1,0:T(4,128)(2,1)} custom-call(bf16[2,256,4,128]{3,2,1,0:T(4,128)(2,1)S(1)} %shard_map.46.o_ref), custom_call_target="tpu_custom_call" | custom-call | tf_op jit(solution)/shard_map/pallas_call | solution.py:453
